TPU v7x, 256 devices: a whole 4x4x8 slice. The times are simulated.
256 devices in a mesh: row: 16 (over z_lo, x), col: 4 (over z_hi, core), depth: 4 (over y).
Axes of the slice: x: 4, y: 4, z: 8 (z_hi: 2, z_lo: 4; z = z_hi * 4 + z_lo), core: 2. Of those that a mesh axis runs over, the one named last changes fastest.
Arguments:
- inputs: bfloat16 [1024, 5120], P(('row', 'depth'), 'col'), may hold values from -6 to 6
- targets: bfloat16 [1024, 5120], P(('row', 'depth'), 'col'), may hold values from -6 to 6
- norm_gain: float32 [5120], P('col'), may hold values from 0.5 to 1.5
- w_gate: bfloat16 [5120, 8192], P('col', ('row', 'depth')), may hold values from -0.078125 to 0.078125
- w_up: bfloat16 [5120, 8192], P('col', ('row', 'depth')), may hold values from -0.078125 to 0.078125
- w_down: bfloat16 [8192, 5120], P(('row', 'depth'), 'col'), may hold values from -0.0625 to 0.0625
- probe_gate: bfloat16 [5120, 8192], P('col', ('row', 'depth')), may hold values from -1 to 1, as said below
- probe_up: bfloat16 [5120, 8192], P('col', ('row', 'depth')), may hold values from -1 to 1, as said below
- probe_down: bfloat16 [8192, 5120], P(('row', 'depth'), 'col'), may hold values from -1 to 1, as said below
- moment_gate: float32 [5120, 8192], P('col', ('row', 'depth')), may hold values from -18 to 18
- moment_up: float32 [5120, 8192], P('col', ('row', 'depth')), may hold values from -18 to 18
- moment_down: float32 [8192, 5120], P(('row', 'depth'), 'col'), may hold values from -18 to 18
- second_gate: float32 [5120, 8192], P('col', ('row', 'depth')), may hold values from 1 to 100
- second_up: float32 [5120, 8192], P('col', ('row', 'depth')), may hold values from 1 to 100
- second_down: float32 [8192, 5120], P(('row', 'depth'), 'col'), may hold values from 1 to 100
Outputs:
- new_moment_gate: float32 [5120, 8192], P('col', ('row', 'depth'))
- new_moment_up: float32 [5120, 8192], P('col', ('row', 'depth'))
- new_moment_down: float32 [8192, 5120], P(('row', 'depth'), 'col')
- new_second_gate: float32 [5120, 8192], P('col', ('row', 'depth'))
- new_second_up: float32 [5120, 8192], P('col', ('row', 'depth'))
- new_second_down: float32 [8192, 5120], P(('row', 'depth'), 'col')
- step_gate: float32 [5120, 8192], P('col', ('row', 'depth'))
- step_up: float32 [5120, 8192], P('col', ('row', 'depth'))
- step_down: float32 [8192, 5120], P(('row', 'depth'), 'col')
Inputs may be any that keep to these rules, and one draw needn't show every extreme that they name: `probe_gate`: every entry is +1 or -1. `probe_up`: every entry is +1 or -1. `probe_down`: every entry is +1 or -1.
All inputs are finite; a program needn't handle non-finite values.
Results may differ from a plain program's by a relative error of at most 0.0046.
Values may be sent and summed in bfloat16 or wider, within the bound.
No kernel may reach another device: no remote copies, remote signals or barrier semaphores. Data moves between devices by JAX's collectives and lax.ppermute only.
A program may use at most 128 MiB of HBM per device.

v0:
```python
import jax
import jax.numpy as jnp
from jax import lax
from jax.sharding import PartitionSpec as P

D = 5120
TILE = 128
STEP = 1000
beta_one = 0.9
beta_two = 0.999
adam_floor = 1e-08
norm_floor = 1e-05


def copy_for_each(value, axis):
    count = lax.axis_size(axis)
    return lax.all_to_all(
        jnp.broadcast_to(value[None], (count, *value.shape)), axis, 0, 0, tiled=True
    )


def of_everyone(value, axis):
    everything = copy_for_each(value, axis)
    return jnp.sum(everything, axis=0)


def cut_along(value, dim, count):
    before, after = (value.shape[:dim], value.shape[dim + 1 :])
    return jnp.moveaxis(value.reshape(*before, count, -1, *after), dim, 0)


def sent_and_summed(value, axis, dim):
    blocks = cut_along(value, dim, lax.axis_size(axis))
    arrived = lax.all_to_all(blocks, axis, split_axis=0, concat_axis=0, tiled=True)
    return arrived.sum(axis=0)


def sent_together(arrays, axis, dim, along):
    widths = [a.shape[along] for a in arrays]
    both = jnp.concatenate(arrays, axis=along)
    result = lax.all_gather(both, axis, axis=dim, tiled=True)
    return tuple(jnp.split(result, [sum(widths[:k]) for k in range(1, len(widths))], axis=along))


def in_one(arrays, axis):
    ends = [0]
    for a in arrays:
        ends.append(ends[-1] + a.size)
    so_far = of_everyone(jnp.concatenate([a.ravel() for a in arrays]), axis)
    return tuple((so_far[b:e].reshape(a.shape) for a, b, e in zip(arrays, ends, ends[1:])))


def silu_parts(gate_pre):
    sig = jax.nn.sigmoid(gate_pre)
    act = gate_pre * sig
    slope = sig * (1.0 + gate_pre * (1.0 - sig))
    bend = sig * (1.0 - sig) * (2.0 + gate_pre * (1.0 - 2.0 * sig))
    return (act, slope, bend)


def tile_means(product):
    height, breadth = product.shape
    blocks = product.reshape(height // TILE, TILE, breadth // TILE, TILE)
    means = jnp.mean(blocks, axis=(1, 3), keepdims=True)
    return jnp.broadcast_to(means, blocks.shape).reshape(height, breadth)


def adahessian(moment, second, gradient, curvature, probe):
    averaged = tile_means(probe.astype(jnp.float32) * curvature)
    new_moment = beta_one * moment + (1.0 - beta_one) * gradient
    new_second = beta_two * second + (1.0 - beta_two) * averaged * averaged
    corrected = new_moment / (1.0 - beta_one**STEP)
    scale_root = jnp.sqrt(new_second / (1.0 - beta_two**STEP))
    return (new_moment, new_second, corrected / (scale_root + adam_floor))


def matmul(left, right):
    return jnp.dot(left, right, preferred_element_type=jnp.float32)


def inner_left(left, right):
    return lax.dot_general(
        left, right, (((0,), (0,)), ((), ())), preferred_element_type=jnp.float32
    )


def inner_right(left, right):
    return lax.dot_general(
        left, right, (((1,), (1,)), ((), ())), preferred_element_type=jnp.float32
    )


def shards(
    inputs,
    targets,
    norm_gain,
    w_gate,
    w_up,
    w_down,
    probe_gate,
    probe_up,
    probe_down,
    moment_gate,
    moment_up,
    moment_down,
    second_gate,
    second_up,
    second_down,
):
    feats = inputs.astype(jnp.float32)
    shard_rows = feats.shape[0]
    local_width = feats.shape[1]
    squares = of_everyone(jnp.sum(feats * feats, axis=1), "col")
    scaling = lax.rsqrt(squares / D + norm_floor)
    normed_rows = (feats * scaling[:, None] * norm_gain).astype(jnp.bfloat16)
    normed = lax.all_gather(normed_rows, ("row", "depth"), axis=0, tiled=True)
    total_rows = normed.shape[0]
    gate_pre, up_pre, gate_tan, up_tan = lax.psum(
        (
            matmul(normed, w_gate),
            matmul(normed, w_up),
            matmul(normed, probe_gate),
            matmul(normed, probe_up),
        ),
        "col",
    )
    act, slope, bend = silu_parts(gate_pre)
    hidden = (act * up_pre).astype(jnp.bfloat16)
    hidden_tan = (slope * gate_tan * up_pre + act * up_tan).astype(jnp.bfloat16)
    row_count = lax.axis_size("row")
    depth_count = lax.axis_size("depth")
    primal = matmul(hidden, w_down)
    tangent = matmul(hidden_tan, w_down) + matmul(hidden, probe_down)
    whole_terms = jnp.concatenate([primal, tangent], axis=1).reshape(
        row_count, depth_count * shard_rows, 2 * local_width
    )
    layered = lax.psum_scatter(whole_terms, "depth", scatter_dimension=1, tiled=True)
    summed = sent_and_summed(layered, "row", 0).reshape(shard_rows, 2 * local_width)
    outputs = summed[:, :local_width] + feats
    error_rows = (outputs - targets.astype(jnp.float32)).astype(jnp.bfloat16)
    tangent_rows = summed[:, local_width:].astype(jnp.bfloat16)
    grid_error, grid_tan = sent_together(
        (
            error_rows.reshape(1, shard_rows, local_width),
            tangent_rows.reshape(1, shard_rows, local_width),
        ),
        "row",
        0,
        1,
    )
    layer_error, layer_tan = sent_together((grid_error, grid_tan), "depth", 1, 0)
    error = layer_error.reshape(total_rows, local_width)
    error_tan = layer_tan.reshape(total_rows, local_width)
    back_hidden, back_tan = in_one(
        (
            inner_right(error, w_down),
            inner_right(error_tan, w_down) + inner_right(error, probe_down),
        ),
        "col",
    )
    back_gate = (back_hidden * up_pre * slope).astype(jnp.bfloat16)
    back_up = (back_hidden * act).astype(jnp.bfloat16)
    gate_tan_back = (
        back_tan * up_pre * slope
        + back_hidden * up_tan * slope
        + back_hidden * up_pre * bend * gate_tan
    ).astype(jnp.bfloat16)
    up_tan_back = (back_tan * act + back_hidden * slope * gate_tan).astype(jnp.bfloat16)
    grad_gate = inner_left(normed, back_gate)
    grad_up = inner_left(normed, back_up)
    grad_down = inner_left(hidden, error)
    curve_gate = inner_left(normed, gate_tan_back)
    curve_up = inner_left(normed, up_tan_back)
    curve_down = inner_left(hidden_tan, error) + inner_left(hidden, error_tan)
    gate_moment, gate_second, gate_step = adahessian(
        moment_gate, second_gate, grad_gate, curve_gate, probe_gate
    )
    up_moment, up_second, up_step = adahessian(moment_up, second_up, grad_up, curve_up, probe_up)
    down_moment, down_second, down_step = adahessian(
        moment_down, second_down, grad_down, curve_down, probe_down
    )
    return (
        gate_moment,
        up_moment,
        down_moment,
        gate_second,
        up_second,
        down_second,
        gate_step,
        up_step,
        down_step,
    )


def solution(mesh):
    return jax.shard_map(
        shards,
        mesh=mesh,
        in_specs=(
            P(("row", "depth"), "col"),
            P(("row", "depth"), "col"),
            P("col"),
            P("col", ("row", "depth")),
            P("col", ("row", "depth")),
            P(("row", "depth"), "col"),
            P("col", ("row", "depth")),
            P("col", ("row", "depth")),
            P(("row", "depth"), "col"),
            P("col", ("row", "depth")),
            P("col", ("row", "depth")),
            P(("row", "depth"), "col"),
            P("col", ("row", "depth")),
            P("col", ("row", "depth")),
            P(("row", "depth"), "col"),
        ),
        out_specs=(
            P("col", ("row", "depth")),
            P("col", ("row", "depth")),
            P(("row", "depth"), "col"),
            P("col", ("row", "depth")),
            P("col", ("row", "depth")),
            P(("row", "depth"), "col"),
            P("col", ("row", "depth")),
            P("col", ("row", "depth")),
            P(("row", "depth"), "col"),
        ),
        check_vma=False,
    )
```

profile of v0, /device:TPU:2, one launch (start us, length us, event | category | flops | bytes accessed | tf_op | source)
XLA Modules:
  0.0 945.6 jit_solution(12996763994163332832)
XLA Ops:
  8.2 15.9 %all_to_all.17 = f32[4,1,16]{2,1,0:T(1,128)S(1)} all-to-all(f32[4,1,16]{2,1,0:T(1,128)S(1)} %broadcast_in_dim.44), channel_id=1, replica_groups=mesh['row'=16,'col'=4,'depth'=4] {'col'}, dimensions={0} | all-to-all | bytes 512 | tf_op jit(solution)/shard_map/all_to_all | solution.py:17
  25.8 342.4 %all-gather.4.cloned.1.call-done = bf16[1024,1280]{1,0:T(8,128)(2,1)} async-done(((bf16[16,1280]{1,0:T(8,128)(2,1)}), bf16[1024,1280]{1,0:T(8,128)(2,1)}) %all-gather.4.cloned.1.call-update) | async-done | bytes 2621456 | tf_op jit(solution)/shard_map/all_gather | solution.py:116
  368.1 3.5 fusion.36
  371.7 1.6 fusion.37
  376.7 99.8 %all-reduce.3.cloned.1.call-done = (f32[1024,128]{1,0:T(8,128)}, f32[1024,128]{1,0:T(8,128)}, f32[1024,128]{1,0:T(8,128)}, f32[1024,128]{1,0:T(8,128)}) async-done(((f32[1024,128]{1,0:T(8,128)}, f32[1024,128]{1,0:T(8,128)}, f32[1024,128]{1,0:T(8,128)}, f32[1024,128]{1,0:T(8,128)}), (f32[1024,128]{1,0:T(8,128)}, f32[1024,128]{1,0:T(8,128)}, f32[1024,128]{1,0:T(8,128)}, ...) | async-done | bytes 2097168 | tf_op jit(solution)/shard_map/psum | solution.py:118
  476.5 1.8 multiply_convert_fusion.2
  479.2 3.1 fusion.38
  482.3 3.2 convolution_add_fusion
  485.5 9.2 pad_maximum_fusion
  494.8 101.7 %reduce-scatter.2.cloned.1.call-done = f32[16,16,2560]{2,1,0:T(8,128)} async-done(((f32[16,64,2560]{2,1,0:T(8,128)}), f32[16,16,2560]{2,1,0:T(8,128)}) %reduce-scatter.2.cloned.1.call-update) | async-done | bytes 2621456 | tf_op jit(solution)/shard_map/reduce_scatter | solution.py:137
  596.5 66.4 %all_to_all.18 = f32[16,1,16,2560]{3,2,1,0:T(8,128)S(1)} all-to-all(f32[16,1,16,2560]{3,2,1,0:T(8,128)} %bitcast.101), channel_id=1, replica_groups=mesh['row'=16,'col'=4,'depth'=4] {'row'}, dimensions={0} | all-to-all | bytes 5242880 | tf_op jit(solution)/shard_map/all_to_all | solution.py:34
  666.2 78.4 %all-gather.6.cloned.1.call-done = bf16[16,32,1280]{2,1,0:T(8,128)(2,1)} async-done(((bf16[1,32,1280]{2,1,0:T(8,128)(2,1)}), bf16[16,32,1280]{2,1,0:T(8,128)(2,1)}) %all-gather.6.cloned.1.call-update) | async-done | bytes 1310736 | tf_op jit(solution)/shard_map/all_gather | solution.py:41
  747.2 58.2 %all-gather.8.cloned.1.call-done = bf16[32,64,1280]{2,1,0:T(8,128)(2,1)} async-done(((bf16[32,16,1280]{2,1,0:T(8,128)(2,1)}), bf16[32,64,1280]{2,1,0:T(8,128)(2,1)}) %all-gather.8.cloned.1.call-update) | async-done | bytes 5242896 | tf_op jit(solution)/shard_map/all_gather | solution.py:41
  805.4 2.9 fusion.34
  811.7 4.6 broadcast_in_dim.45
  816.3 7.0 all-to-all-start.2
  823.3 1.9 copy.33
  825.2 1.9 copy.32
  830.1 2.0 add_divide_fusion
  832.2 87.5 %all-to-all-done.2 = f32[4,1,262144]{2,1,0:T(1,128)} async-done(((f32[4,1,262144]{2,1,0:T(1,128)}), f32[4,1,262144]{2,1,0:T(1,128)}, u32[]{:S(2)}, u32[]{:S(2)}) %all-to-all-start.2) | async-done | bytes 4194336 | tf_op jit(solution)/shard_map/all_to_all | solution.py:17
  919.7 10.8 %reduce_sum.87 = f32[262144]{0:T(1024)} reduce(f32[4,1,262144]{2,1,0:T(1,128)} %all-to-all-done.2, f32[]{:T(128)} %constant.13.clone.1), dimensions={0,1}, to_apply=%region_8.0 | reduce | flops 786432 | bytes 5242884 | tf_op jit(solution)/shard_map/reduce_sum | solution.py:24
  930.5 2.2 fusion.7
  934.3 2.4 add_divide_fusion.1
  936.6 2.4 add_divide_fusion.2
  (92 shorter events, 20.7 us)
Async XLA Ops:
  7.2 471.2 %copy-start = (bf16[128,1280]{1,0:T(8,128)(2,1)S(1)}, bf16[128,1280]{1,0:T(8,128)(2,1)}, u32[]{:S(2)}) copy-start(bf16[128,1280]{1,0:T(8,128)(2,1)} %param.20) | copy-start | bytes 983044
  7.2 364.5 %copy-start.19 = (bf16[1280,128]{1,0:T(8,128)(2,1)S(1)}, bf16[1280,128]{1,0:T(8,128)(2,1)}, u32[]{:S(2)}) copy-start(bf16[1280,128]{1,0:T(8,128)(2,1)} %param.19) | copy-start | bytes 983044
  7.2 360.9 %all-gather.4.cloned.1.call-start = ((), (), s32[]{:S(2)}) async-start(), calls=%async_computation.4 | async-start | bytes 2662400 | tf_op jit(solution)/shard_map/all_gather | solution.py:116
  25.7 450.8 %all-reduce.3.cloned.1.call-start = ((), (), s32[]{:S(2)}) async-start(), calls=%async_computation.8 | async-start | bytes 4194304 | tf_op jit(solution)/shard_map/psum | solution.py:118
  368.1 3.6 copy-start.2
  376.6 219.8 %reduce-scatter.2.cloned.1.call-start = ((), (), s32[]{:S(2)}) async-start(), calls=%async_computation.5 | async-start | bytes 13107200 | tf_op jit(solution)/shard_map/reduce_scatter | solution.py:137
  479.2 3.1 copy-start.6
  494.7 249.9 %all-gather.6.cloned.1.call-start = ((), (), s32[]{:S(2)}) async-start(), calls=%async_computation.6 | async-start | bytes 1392640 | tf_op jit(solution)/shard_map/all_gather | solution.py:41
  662.9 1.7 copy-start.18
  662.9 1.7 copy-start.21
  666.1 139.3 %all-gather.8.cloned.1.call-start = ((), (), s32[]{:S(2)}) async-start(), calls=%async_computation.7 | async-start | bytes 6553600 | tf_op jit(solution)/shard_map/all_gather | solution.py:41
  816.3 103.4 %all-to-all-start.2 = ((f32[4,1,262144]{2,1,0:T(1,128)}), f32[4,1,262144]{2,1,0:T(1,128)}, u32[]{:S(2)}, u32[]{:S(2)}) async-start(f32[4,1,262144]{2,1,0:T(1,128)} %broadcast_in_dim.45), calls=%async_computation.3 | async-start | bytes 8388608 | tf_op jit(solution)/shard_map/all_to_all | solution.py:17
  823.3 4.3 copy-start.8
  827.1 1.7 copy-start.5
  832.2 98.3 %copy-start.3 = (bf16[1024,1280]{1,0:T(8,128)(2,1)S(1)}, bf16[1024,1280]{1,0:T(8,128)(2,1)}, u32[]{:S(2)}) copy-start(bf16[1024,1280]{1,0:T(8,128)(2,1)} %all-gather.4.cloned.1.call-done) | copy-start | bytes 7864324
  832.2 98.3 %copy-start.15 = (f32[1024,128]{1,0:T(8,128)S(1)}, f32[1024,128]{1,0:T(8,128)}, u32[]{:S(2)}) copy-start(f32[1024,128]{1,0:T(8,128)} %get-tuple-element.12) | copy-start | bytes 1572868
  930.5 2.5 copy-start.11
  930.5 2.5 copy-start.14
  930.5 2.5 copy-start.16
  930.5 2.5 copy-start.17
  930.5 2.5 copy-start.20
  934.3 2.4 copy-start.24
  934.3 2.4 copy-start.25
  936.6 2.4 copy-start.1
  (8 other events, 10.6 us)
Sparse Core Ops, SparseCore 0:
  25.8 342.2 all-gather.3
  376.8 99.7 all-reduce.2
  494.8 101.5 reduce-scatter.1
  666.3 78.3 all-gather.5
  747.3 57.9 all-gather.7
where the time goes:
time: 946 us
  waiting for transfers between devices  768 us (81%)
  blocking collectives  82.3 us (9%)
  matrix products  29.1 us (3%)
  other arithmetic  28.5 us (3%)
  local copies, waits for them, and re-layouts  16.4 us (2%)
  between operations  14 us (1%)
    all_gather x1, waiting for transfers between devices, shards(): normed = lax.all_gather(normed_rows, ('row', 'depth'), axis=0, tiled=True)  342 us
    all_gather x2, waiting for transfers between devices, sent_together(): result = lax.all_gather(both, axis, axis=dim, tiled=True)  137 us
    reduce_scatter x1, waiting for transfers between devices, shards(): lax.psum_scatter(whole_terms, 'depth', scatter_dimension=1, tiled=True)  102 us
    psum x1, waiting for transfers between devices, shards(): lax.psum((matmul(normed, w_gate), matmul(normed, w_up), matmul(normed, pr...  99.8 us
    all_to_all x1, waiting for transfers between devices, copy_for_each(): lax.all_to_all(jnp.broadcast_to(value[None], (count, *value.shape)), axis...  87.5 us
    all_to_all x1, blocking collectives, sent_and_summed(): lax.all_to_all(blocks, axis, split_axis=0, concat_axis=0, tiled=True)  66.4 us
  transfers between devices with their start and end apart: 6, of which 6 were waited for; matrix products, arithmetic and copies ran while one was open for 1% of the time, Pallas kernels for 0%

commit v1 on v0

--- a/solution.py
+++ b/solution.py
@@ -113,7 +113,10 @@
     squares = of_everyone(jnp.sum(feats * feats, axis=1), "col")
     scaling = lax.rsqrt(squares / D + norm_floor)
     normed_rows = (feats * scaling[:, None] * norm_gain).astype(jnp.bfloat16)
-    normed = lax.all_gather(normed_rows, ("row", "depth"), axis=0, tiled=True)
+    size = lax.axis_size(("row", "depth"))
+    pieces = jnp.stack([normed_rows for _ in range(size)])
+    pieces = lax.all_to_all(pieces, ("row", "depth"), split_axis=0, concat_axis=0)
+    normed = jnp.concatenate(pieces, axis=0)
     total_rows = normed.shape[0]
     gate_pre, up_pre, gate_tan, up_tan = lax.psum(
         (

time: 946 us -> 665 us (0.70)
  waiting for transfers between devices: 768 us -> 416 us
  blocking collectives: 82.3 us -> 152 us
    all_gather x1 -> x0, waiting for transfers between devices: 342 us -> none  [shards(): normed = lax.all_gather(normed_rows, ('row', 'depth'), axis=0, tiled=True)]
    all_to_all x0 -> x1, blocking collectives: none -> 70 us  [shards(): lax.all_to_all(pieces, ('row', 'depth'), split_axis=0, concat_axis=0)]
  transfers between devices with their start and end apart: 6 -> 5, of which waited for: 6 -> 5; matrix products, arithmetic and copies ran while one was open for 1% -> 1% of each run, Pallas kernels for 0% -> 0%
where the time goes in v1:
time: 665 us
  waiting for transfers between devices  416 us (63%)
  blocking collectives  152 us (23%)
  other arithmetic  29.6 us (4%)
  matrix products  29.1 us (4%)
  local copies, waits for them, and re-layouts  16.3 us (2%)
  between operations  14 us (2%)
  starting transfers between devices  7.17 us (1%)
    all_gather x2, waiting for transfers between devices, sent_together(): result = lax.all_gather(both, axis, axis=dim, tiled=True)  137 us
    reduce_scatter x1, waiting for transfers between devices, shards(): lax.psum_scatter(whole_terms, 'depth', scatter_dimension=1, tiled=True)  102 us
    psum x1, waiting for transfers between devices, shards(): lax.psum((matmul(normed, w_gate), matmul(normed, w_up), matmul(normed, pr...  91.7 us
    all_to_all x1, waiting for transfers between devices, copy_for_each(): lax.all_to_all(jnp.broadcast_to(value[None], (count, *value.shape)), axis...  86.1 us
    all_to_all x1, blocking collectives, shards(): lax.all_to_all(pieces, ('row', 'depth'), split_axis=0, concat_axis=0)  70 us
    all_to_all x1, blocking collectives, sent_and_summed(): lax.all_to_all(blocks, axis, split_axis=0, concat_axis=0, tiled=True)  66.5 us
    all_to_all x1, blocking collectives, copy_for_each(): lax.all_to_all(jnp.broadcast_to(value[None], (count, *value.shape)), axis...  15.9 us
    dot_general x7, matrix products, matmul(): return jnp.dot(left, right, preferred_element_type=jnp.float32)  13.6 us
  transfers between devices with their start and end apart: 5, of which 5 were waited for; matrix products, arithmetic and copies ran while one was open for 1% of the time, Pallas kernels for 0%

profile of v1, /device:TPU:2, one launch (start us, length us, event | category | flops | bytes accessed | tf_op | source)
XLA Modules:
  0.0 664.7 jit_solution(411793362196336059)
XLA Ops:
  8.2 15.9 %all_to_all.22 = f32[4,1,16]{2,1,0:T(1,128)S(1)} all-to-all(f32[4,1,16]{2,1,0:T(1,128)S(1)} %broadcast_in_dim.44), channel_id=1, replica_groups=mesh['row'=16,'col'=4,'depth'=4] {'col'}, dimensions={0} | all-to-all | bytes 512 | tf_op jit(solution)/shard_map/all_to_all | solution.py:17
  25.2 70.0 %all_to_all.23 = bf16[64,16,1280]{2,1,0:T(8,128)(2,1)S(1)} all-to-all(bf16[64,16,1280]{2,1,0:T(8,128)(2,1)S(1)} %stack.2), channel_id=1, replica_groups=mesh['row'=16,'col'=4,'depth'=4] {'row','depth'}, dimensions={0} | all-to-all | bytes 5242880 | tf_op jit(solution)/shard_map/all_to_all | solution.py:118
  101.9 91.7 %all-reduce.3.cloned.1.call-done = (f32[1024,128]{1,0:T(8,128)}, f32[1024,128]{1,0:T(8,128)}, f32[1024,128]{1,0:T(8,128)}, f32[1024,128]{1,0:T(8,128)}) async-done(((f32[1024,128]{1,0:T(8,128)}, f32[1024,128]{1,0:T(8,128)}, f32[1024,128]{1,0:T(8,128)}, f32[1024,128]{1,0:T(8,128)}), (f32[1024,128]{1,0:T(8,128)}, f32[1024,128]{1,0:T(8,128)}, f32[1024,128]{1,0:T(8,128)}, ...) | async-done | bytes 2097168 | tf_op jit(solution)/shard_map/psum | solution.py:121
  193.5 1.8 multiply_convert_fusion.2
  196.2 3.1 fusion.38
  199.3 3.2 convolution_add_fusion
  202.5 9.2 %pad_maximum_fusion = f32[1024,2560]{1,0:T(8,128)} fusion(f32[1024,1280]{1,0:T(8,128)} %convolution_add_fusion, f32[1024,1280]{1,0:T(8,128)} %fusion.38), kind=kLoop, calls=%fused_computation.1 | loop fusion | flops 2621440 | bytes 20971520 | tf_op jit(solution)/shard_map/concatenate | solution.py:137
  211.8 101.7 %reduce-scatter.2.cloned.1.call-done = f32[16,16,2560]{2,1,0:T(8,128)} async-done(((f32[16,64,2560]{2,1,0:T(8,128)}), f32[16,16,2560]{2,1,0:T(8,128)}) %reduce-scatter.2.cloned.1.call-update) | async-done | bytes 2621456 | tf_op jit(solution)/shard_map/reduce_scatter | solution.py:140
  313.5 66.5 %all_to_all.24 = f32[16,1,16,2560]{3,2,1,0:T(8,128)} all-to-all(f32[16,1,16,2560]{3,2,1,0:T(8,128)} %bitcast.110), channel_id=1, replica_groups=mesh['row'=16,'col'=4,'depth'=4] {'row'}, dimensions={0} | all-to-all | bytes 5242880 | tf_op jit(solution)/shard_map/all_to_all | solution.py:34
  380.0 2.6 reduce_sum.86
  385.1 78.4 %all-gather.3.cloned.1.call-done = bf16[16,32,1280]{2,1,0:T(8,128)(2,1)} async-done(((bf16[1,32,1280]{2,1,0:T(8,128)(2,1)}), bf16[16,32,1280]{2,1,0:T(8,128)(2,1)}) %all-gather.3.cloned.1.call-update) | async-done | bytes 1310736 | tf_op jit(solution)/shard_map/all_gather | solution.py:41
  466.1 58.2 %all-gather.5.cloned.1.call-done = bf16[32,64,1280]{2,1,0:T(8,128)(2,1)} async-done(((bf16[32,16,1280]{2,1,0:T(8,128)(2,1)}), bf16[32,64,1280]{2,1,0:T(8,128)(2,1)}) %all-gather.5.cloned.1.call-update) | async-done | bytes 5242896 | tf_op jit(solution)/shard_map/all_gather | solution.py:41
  524.3 2.9 fusion.34
  530.8 4.6 broadcast_in_dim.45
  535.4 7.0 %all-to-all-start.3 = ((f32[4,1,262144]{2,1,0:T(1,128)}), f32[4,1,262144]{2,1,0:T(1,128)}, u32[]{:S(2)}, u32[]{:S(2)}) async-start(f32[4,1,262144]{2,1,0:T(1,128)} %broadcast_in_dim.45), calls=%async_computation.4 | async-start | bytes 8388608 | tf_op jit(solution)/shard_map/all_to_all | solution.py:17
  542.4 1.9 copy.33
  544.3 1.9 copy.32
  546.2 2.4 fusion.43
  550.7 2.1 add_divide_fusion
  552.7 86.1 %all-to-all-done.3 = f32[4,1,262144]{2,1,0:T(1,128)} async-done(((f32[4,1,262144]{2,1,0:T(1,128)}), f32[4,1,262144]{2,1,0:T(1,128)}, u32[]{:S(2)}, u32[]{:S(2)}) %all-to-all-start.3) | async-done | bytes 4194336 | tf_op jit(solution)/shard_map/all_to_all | solution.py:17
  638.8 10.8 %reduce_sum.87 = f32[262144]{0:T(1024)} reduce(f32[4,1,262144]{2,1,0:T(1,128)} %all-to-all-done.3, f32[]{:T(128)} %constant.13.clone.1), dimensions={0,1}, to_apply=%region_8.0 | reduce | flops 786432 | bytes 5242884 | tf_op jit(solution)/shard_map/reduce_sum | solution.py:24
  649.6 2.2 fusion.7
  653.4 2.4 add_divide_fusion.1
  655.7 2.4 add_divide_fusion.2
  (93 shorter events, 21.8 us)
Async XLA Ops:
  7.2 188.2 %copy-start = (bf16[128,1280]{1,0:T(8,128)(2,1)S(1)}, bf16[128,1280]{1,0:T(8,128)(2,1)}, u32[]{:S(2)}) copy-start(bf16[128,1280]{1,0:T(8,128)(2,1)} %param.20) | copy-start | bytes 983044
  7.2 186.4 %all-reduce.3.cloned.1.call-start = ((), (), s32[]{:S(2)}) async-start(), calls=%async_computation.8 | async-start | bytes 4194304 | tf_op jit(solution)/shard_map/psum | solution.py:121
  25.2 70.0 %copy-start.19 = (bf16[1280,128]{1,0:T(8,128)(2,1)S(1)}, bf16[1280,128]{1,0:T(8,128)(2,1)}, u32[]{:S(2)}) copy-start(bf16[1280,128]{1,0:T(8,128)(2,1)} %param.18) | copy-start | bytes 983044
  101.8 211.6 %reduce-scatter.2.cloned.1.call-start = ((), (), s32[]{:S(2)}) async-start(), calls=%async_computation.5 | async-start | bytes 13107200 | tf_op jit(solution)/shard_map/reduce_scatter | solution.py:140
  196.2 3.1 copy-start.6
  211.7 251.8 %all-gather.3.cloned.1.call-start = ((), (), s32[]{:S(2)}) async-start(), calls=%async_computation.6 | async-start | bytes 1392640 | tf_op jit(solution)/shard_map/all_gather | solution.py:41
  380.0 3.5 copy-start.18
  380.0 3.5 copy-start.22
  385.0 139.3 %all-gather.5.cloned.1.call-start = ((), (), s32[]{:S(2)}) async-start(), calls=%async_computation.7 | async-start | bytes 6553600 | tf_op jit(solution)/shard_map/all_gather | solution.py:41
  527.2 2.4 copy-start.2
  535.4 103.4 %all-to-all-start.3 = ((f32[4,1,262144]{2,1,0:T(1,128)}), f32[4,1,262144]{2,1,0:T(1,128)}, u32[]{:S(2)}, u32[]{:S(2)}) async-start(f32[4,1,262144]{2,1,0:T(1,128)} %broadcast_in_dim.45), calls=%async_computation.4 | async-start | bytes 8388608 | tf_op jit(solution)/shard_map/all_to_all | solution.py:17
  542.4 6.2 copy-start.8
  546.2 2.5 copy-start.5
  546.2 3.3 copy-start.13
  548.7 1.9 copy-start.12
  552.7 96.9 %copy-start.15 = (f32[1024,128]{1,0:T(8,128)S(1)}, f32[1024,128]{1,0:T(8,128)}, u32[]{:S(2)}) copy-start(f32[1024,128]{1,0:T(8,128)} %get-tuple-element.12) | copy-start | bytes 1572868
  649.6 2.5 copy-start.11
  649.6 2.5 copy-start.14
  649.6 2.5 copy-start.16
  649.6 2.5 copy-start.17
  649.6 2.5 copy-start.21
  653.4 2.4 copy-start.25
  653.4 2.4 copy-start.26
  655.7 2.4 copy-start.1
  (8 other events, 11.8 us)
Sparse Core Ops, SparseCore 0:
  102.0 91.5 all-reduce.2
  211.8 101.5 reduce-scatter.1
  385.1 78.3 all-gather.2
  466.2 57.9 all-gather.4
